TPU v7x, 32 devices: a whole 2x2x4 slice. The times are simulated.
32 devices in a mesh: dp: 16 (over z, y, core), mp: 2 (over x).
Axes of the slice: x: 2, y: 2, z: 4, core: 2. Of those that a mesh axis runs over, the one named last changes fastest.
Arguments:
- activations: bfloat16 [8192, 1792], P('dp', 'mp'), may hold values from -6 to 6
- projection: bfloat16 [1792, 9216], P('mp', 'dp'), may hold values from -0.125 to 0.125
Outputs:
- projected: bfloat16 [8192, 9216], P('dp', 'mp')
All inputs are finite; a program needn't handle non-finite values.
Results may differ from a plain program's by a relative error of at most 0.001.
Values may be sent and summed in bfloat16 or wider, within the bound.
A program may use at most 128 MiB of HBM per device.

v0:
```python
import jax
import jax.numpy as jnp
from jax import lax
from jax.sharding import PartitionSpec as P


def shards(activations, projection):
    wide_rows = lax.all_gather(activations, "mp", axis=1, tiled=True)
    local_cols = lax.all_to_all(projection, "mp", split_axis=1, concat_axis=0, tiled=True)
    finished = jnp.dot(
        wide_rows,
        lax.all_gather(local_cols, "dp", axis=1, tiled=True),
        preferred_element_type=jnp.float32,
    )
    finished = finished.astype(jnp.bfloat16)
    tok_rows = finished.shape[0]
    blocks = lax.axis_size("dp")
    share = local_cols.shape[1]
    sectioned = finished.reshape(tok_rows, blocks, 1, share)
    placed = lax.all_to_all(sectioned, "mp", split_axis=1, concat_axis=2, tiled=True)
    return placed.reshape(tok_rows, placed.shape[1] * placed.shape[2] * share)


def solution(mesh):
    placed = (P("dp", "mp"), P("mp", "dp"))
    return jax.shard_map(
        shards, mesh=mesh, in_specs=placed, out_specs=P("dp", "mp"), check_vma=False
    )
```

profile of v0, /device:TPU:3, one launch (start us, length us, event | category | flops | bytes accessed | tf_op | source)
XLA Modules:
  0.0 265.1 jit_solution(4913210629875700962)
XLA Ops:
  6.5 0.0 all-gather.3.cloned.1.call-start
  6.5 0.7 all-gather.3.cloned.1.call-update
  7.3 0.0 all-gather.5.cloned.1.call-start
  7.3 17.5 %all_to_all.34 = bf16[896,2,288]{0,2,1:T(8,128)(2,1)S(1)} all-to-all(bf16[896,2,288]{0,2,1:T(8,128)(2,1)} %bitcast.18), channel_id=1, replica_groups=mesh['dp'=16,'mp'=2] {'mp'}, dimensions={1} | all-to-all | bytes 2064384 | tf_op jit(solution)/shard_map/all_to_all | solution.py:9
  24.8 1.0 copy.17
  25.9 0.0 all-gather.5.cloned.1.call-update
  25.9 16.7 %all-gather.3.cloned.1.call-done = bf16[512,1792]{1,0:T(8,128)(2,1)} async-done(((bf16[512,896]{1,0:T(8,128)(2,1)}), bf16[512,1792]{1,0:T(8,128)(2,1)}) %all-gather.3.cloned.1.call-update) | async-done | bytes 1835024 | tf_op jit(solution)/shard_map/all_gather | solution.py:8
  42.6 129.6 %all-gather.5.cloned.1.call-done = bf16[1792,4608]{0,1:T(8,128)(2,1)} async-done(((bf16[1792,288]{0,1:T(8,128)(2,1)}), bf16[1792,4608]{0,1:T(8,128)(2,1)}) %all-gather.5.cloned.1.call-update) | async-done | bytes 16515088 | tf_op jit(solution)/shard_map/all_gather | solution.py:12
  172.3 14.2 %convolution_convert_fusion = bf16[512,4608]{1,0:T(8,128)(2,1)} fusion(bf16[512,1792]{1,0:T(8,128)(2,1)} %all-gather.3.cloned.1.call-done, bf16[1792,4608]{0,1:T(8,128)(2,1)} %all-gather.5.cloned.1.call-done), kind=kOutput, calls=%fused_computation | convolution fusion | flops 8458076160 | bytes 23068672 | tf_op jit(solution)/shard_map/dot_general | solution.py:10
  186.5 6.7 %copy.13 = bf16[512,4608]{0,1:T(8,128)(2,1)} copy(bf16[512,4608]{1,0:T(8,128)(2,1)} %convolution_convert_fusion) | data formatting | bytes 9437184 | tf_op jit(solution)/shard_map/convert_element_type | solution.py:15
  193.1 56.1 %all_to_all.35 = bf16[512,16,1,288]{0,3,2,1:T(8,128)(2,1)S(1)} all-to-all(bf16[512,16,1,288]{0,3,2,1:T(8,128)(2,1)} %bitcast.13), channel_id=1, replica_groups=mesh['dp'=16,'mp'=2] {'mp'}, dimensions={1} | all-to-all | bytes 9437184 | tf_op jit(solution)/shard_map/all_to_all | solution.py:20
  249.2 2.4 copy.15
  251.6 6.6 %copy.16 = bf16[512,4608]{1,0:T(8,128)(2,1)} copy(bf16[512,4608]{0,1:T(8,128)(2,1)} %bitcast.15) | data formatting | bytes 9437184 | tf_op jit(solution)/shard_map/reshape | solution.py:21
Async XLA Ops:
  6.5 36.1 %all-gather.3.cloned.1.call-start = ((), (), s32[]{:S(2)}) async-start(), calls=%async_computation.2 | async-start | bytes 2752512 | tf_op jit(solution)/shard_map/all_gather | solution.py:8
  7.3 165.0 %all-gather.5.cloned.1.call-start = ((), (), s32[]{:S(2)}) async-start(), calls=%async_computation.3 | async-start | bytes 17547264 | tf_op jit(solution)/shard_map/all_gather | solution.py:12
Sparse Core Ops, SparseCore 0:
  8.9 33.7 all-gather.2
  44.9 127.3 all-gather.4
where the time goes:
time: 268 us; the launch traced here: 265 us
  waiting for transfers between devices  147 us (55%)
  blocking collectives  73.6 us (27%)
  local copies, waits for them, and re-layouts  16.7 us (6%)
  matrix products  14.2 us (5%)
  between operations  13.4 us (5%)
    all_gather x1, waiting for transfers between devices, shards(): lax.all_gather(local_cols, 'dp', axis=1, tiled=True)  130 us
    all_to_all x1, blocking collectives, shards(): lax.all_to_all(sectioned, 'mp', split_axis=1, concat_axis=2, tiled=True)  56.1 us
    all_to_all x1, blocking collectives, shards(): lax.all_to_all(projection, 'mp', split_axis=1, concat_axis=0, tiled=True)  17.5 us
    all_gather x1, waiting for transfers between devices, shards(): wide_rows = lax.all_gather(activations, 'mp', axis=1, tiled=True)  16.7 us
    dot_general x1, matrix products, shards(): jnp.dot(wide_rows, lax.all_gather(local_cols, 'dp', axis=1, tiled=True),...  14.2 us
    convert_element_type x1, local copies, waits for them, and re-layouts, shards(): finished = finished.astype(jnp.bfloat16)  6.66 us
    reshape x1, local copies, waits for them, and re-layouts, shards(): return placed.reshape(tok_rows, placed.shape[1] * placed.shape[2] * share)  6.61 us
  transfers between devices with their start and end apart: 2, of which 2 were waited for; matrix products, arithmetic and copies ran while one was open for 0% of the time, Pallas kernels for 0%

commit v1 on v0

--- a/solution.py
+++ b/solution.py
@@ -1,10 +1,19 @@
+import functools
+
 import jax
 import jax.numpy as jnp
 from jax import lax
+from jax.experimental import pallas as pl
+from jax.experimental.pallas import tpu as pltpu
 from jax.sharding import PartitionSpec as P
 
-
-def shards(activations, projection):
+MESH = pl.DeviceIdType.MESH
+LANES = 128
+ACT_PIECES = 4
+MM_LAG = 4
+
+
+def general(activations, projection):
     wide_rows = lax.all_gather(activations, "mp", axis=1, tiled=True)
     local_cols = lax.all_to_all(projection, "mp", split_axis=1, concat_axis=0, tiled=True)
     finished = jnp.dot(
@@ -21,7 +30,251 @@
     return placed.reshape(tok_rows, placed.shape[1] * placed.shape[2] * share)
 
 
+def kernel(nz, a_ref, w_ref, o_ref, big, acts, stage, outs, send_sem, recv_sem,
+           act_send, act_recv, loc_sem, stage_sem, out_sem):
+    d, x = lax.axis_index("dp"), lax.axis_index("mp")
+    z, y, c = d // 4, (d // 2) % 2, d % 2
+    half = nz // 2
+    pair = big.shape[2]
+    depth = w_ref.shape[0]
+    part = depth // 2
+    steps = pair // LANES
+    rows = a_ref.shape[0]
+    lane = x * 2 + c
+    core_dev = (d + 1 - 2 * c, x)
+    y_dev = (d + 2 - 4 * y, x)
+    x_dev = (d, 1 - x)
+    up_dev = (lax.rem(d + 4, 4 * nz), x)
+    down_dev = (lax.rem(d + 4 * nz - 4, 4 * nz), x)
+    can_up, can_down = z < nz - 1, z > 0
+
+    own_act = pltpu.make_async_copy(
+        a_ref, acts.at[:, pl.ds(pl.multiple_of(x * depth, LANES), depth)], loc_sem.at[0])
+    own_act.start()
+    mine_rows = pltpu.make_async_copy(
+        w_ref.at[pl.ds(pl.multiple_of(c * part, 16), part), :], stage.at[c], loc_sem.at[1])
+    mine_rows.start()
+
+    barrier = pltpu.get_barrier_semaphore()
+    for dev in (core_dev, y_dev, x_dev):
+        pl.semaphore_signal(barrier, inc=1, device_id=dev, device_id_type=MESH)
+
+    @pl.when(can_up)
+    def _():
+        pl.semaphore_signal(barrier, inc=1, device_id=up_dev, device_id_type=MESH)
+
+    @pl.when(can_down)
+    def _():
+        pl.semaphore_signal(barrier, inc=1, device_id=down_dev, device_id_type=MESH)
+
+    pl.semaphore_wait(barrier, 3 + can_up.astype(jnp.int32) + can_down.astype(jnp.int32))
+
+    swap = pltpu.make_async_remote_copy(
+        src_ref=w_ref.at[pl.ds(pl.multiple_of((1 - c) * part, 16), part), :],
+        dst_ref=stage.at[c], send_sem=stage_sem.at[0], recv_sem=stage_sem.at[1],
+        device_id=core_dev, device_id_type=MESH)
+    swap.start()
+    mine_rows.wait()
+    swap.wait()
+    big[z * 2 + y, pl.ds(pl.multiple_of(lane * part, 16), part), :] = jnp.concatenate(
+        [stage[0], stage[1]], axis=1)
+
+    def copy(kind, zz, yy, q, s, dev):
+        piece = big.at[zz * 2 + yy, pl.ds(pl.multiple_of(q * part, 16), part),
+                       pl.ds(pl.multiple_of(s * LANES, LANES), LANES)]
+        return pltpu.make_async_remote_copy(
+            src_ref=piece, dst_ref=piece, send_sem=send_sem.at[kind, zz, s],
+            recv_sem=recv_sem.at[zz, yy, q, s], device_id=dev, device_id_type=MESH)
+
+    def z_stage(s, act, arrive):
+        def lane_piece(zz, up, down):
+            @pl.when(up)
+            def _():
+                act(copy(0, zz, y, lane, s, up_dev))
+
+            @pl.when(down)
+            def _():
+                act(copy(1, zz, y, lane, s, down_dev))
+
+            @pl.when(zz // half == x)
+            def _():
+                act(copy(2, zz, y, lane, s, y_dev))
+                act(copy(3, zz, y, lane, s, core_dev))
+
+            @pl.when(zz // half != x)
+            def _():
+                act(copy(2, zz, y, lane, s, x_dev))
+
+        lane_piece(z, can_up, can_down)
+        for dist in range(1, nz):
+            @pl.when(z >= dist)
+            def _():
+                arrive(z - dist, y, lane, s)
+                lane_piece(z - dist, can_up, z < 0)
+
+            @pl.when(z + dist < nz)
+            def _():
+                arrive(z + dist, y, lane, s)
+                lane_piece(z + dist, z < 0, can_down)
+
+    def x_stage(s, act, arrive):
+        for h in range(half):
+            zz, q = x * half + h, (1 - x) * 2 + c
+            arrive(zz, y, q, s)
+            act(copy(4, zz, y, q, s, y_dev))
+            act(copy(5, zz, y, q, s, core_dev))
+
+    def y_stage(s, act, arrive):
+        for h in range(half):
+            for xx in range(2):
+                zz, q = x * half + h, xx * 2 + c
+                arrive(zz, 1 - y, q, s)
+                act(copy(6 + xx, zz, 1 - y, q, s, core_dev))
+
+    def core_stage(s, arrive):
+        for h in range(half):
+            for yy in range(2):
+                for xx in range(2):
+                    arrive(x * half + h, yy, xx * 2 + 1 - c, s)
+
+    def start(cp):
+        cp.start()
+
+    def drain(cp):
+        cp.wait_send()
+
+    def arrive(zz, yy, q, s):
+        copy(0, zz, yy, q, s, core_dev).wait_recv()
+
+    def no_arrive(zz, yy, q, s):
+        pass
+
+    act_rows = rows // ACT_PIECES
+
+    def act_copy(k):
+        piece = pl.ds(pl.multiple_of(k * act_rows, 16), act_rows)
+        return pltpu.make_async_remote_copy(
+            src_ref=a_ref.at[piece, :],
+            dst_ref=acts.at[piece, pl.ds(pl.multiple_of(x * depth, LANES), depth)],
+            send_sem=act_send.at[k], recv_sem=act_recv.at[k],
+            device_id=x_dev, device_id_type=MESH)
+
+    def act_in(k):
+        piece = pl.ds(pl.multiple_of(k * act_rows, 16), act_rows)
+        return pltpu.make_async_remote_copy(
+            src_ref=a_ref.at[piece, :],
+            dst_ref=acts.at[piece, pl.ds(pl.multiple_of((1 - x) * depth, LANES), depth)],
+            send_sem=act_send.at[k], recv_sem=act_recv.at[k],
+            device_id=x_dev, device_id_type=MESH)
+
+    def out_copy(b, s):
+        cols = pl.ds(pl.multiple_of(b * pair + s * LANES, LANES), LANES)
+        return pltpu.make_async_copy(outs.at[:, cols], o_ref.at[:, cols], out_sem.at[b, s])
+
+    def multiply(s):
+        cols = pl.ds(pl.multiple_of(s * LANES, LANES), LANES)
+        for b in range(0, 2 * half, 2):
+            base = x * 2 * half + b
+            rhs = jnp.concatenate([big[base, :, cols], big[base + 1, :, cols]], axis=1)
+            res = jnp.dot(acts[...], rhs, preferred_element_type=jnp.float32).astype(jnp.bfloat16)
+            for k in range(2):
+                at = pl.ds(pl.multiple_of((b + k) * pair + s * LANES, LANES), LANES)
+                outs[:, at] = res[:, k * LANES:(k + 1) * LANES]
+                out_copy(b + k, s).start()
+
+    def within(s):
+        return jnp.logical_and(s >= 0, s < steps)
+
+    def step(i, carry):
+        @pl.when(within(i))
+        def _():
+            z_stage(i, start, arrive)
+
+        @pl.when(i < ACT_PIECES)
+        def _():
+            act_copy(i).start()
+
+        @pl.when(within(i - 1))
+        def _():
+            x_stage(i - 1, start, arrive)
+
+        @pl.when(within(i - 2))
+        def _():
+            y_stage(i - 2, start, arrive)
+
+        @pl.when(i == MM_LAG)
+        def _():
+            own_act.wait()
+            for k in range(ACT_PIECES):
+                act_in(k).wait_recv()
+
+        @pl.when(within(i - MM_LAG))
+        def _():
+            core_stage(i - MM_LAG, arrive)
+            multiply(i - MM_LAG)
+
+        return carry
+
+    lax.fori_loop(0, steps + MM_LAG, step, 0)
+
+    def finish(s, carry):
+        z_stage(s, drain, no_arrive)
+        x_stage(s, drain, no_arrive)
+        y_stage(s, drain, no_arrive)
+        for b in range(2 * half):
+            out_copy(b, s).wait()
+        return carry
+
+    lax.fori_loop(0, steps, finish, 0)
+    for k in range(ACT_PIECES):
+        act_copy(k).wait_send()
+
+
+def gathered(nz, activations, projection):
+    rows, depth = activations.shape
+    width = projection.shape[1]
+    pair, steps, half = 2 * width, 2 * width // LANES, nz // 2
+    columns = nz * 2 * pair // 2
+    dma = pltpu.SemaphoreType.DMA
+    return pl.pallas_call(
+        functools.partial(kernel, nz),
+        out_shape=jax.ShapeDtypeStruct((rows, columns), jnp.bfloat16),
+        in_specs=[pl.BlockSpec(memory_space=pl.ANY)] * 2,
+        out_specs=pl.BlockSpec(memory_space=pl.ANY),
+        scratch_shapes=[
+            pltpu.VMEM((nz * 2, 2 * depth, pair), jnp.bfloat16),
+            pltpu.VMEM((rows, 2 * depth), jnp.bfloat16),
+            pltpu.VMEM((2, depth // 2, width), jnp.bfloat16),
+            pltpu.VMEM((rows, columns), jnp.bfloat16),
+            dma((8, nz, steps)),
+            dma((nz, 2, 4, steps)),
+            dma((ACT_PIECES,)),
+            dma((ACT_PIECES,)),
+            dma((2,)),
+            dma((2,)),
+            dma((2 * half, steps)),
+        ],
+        compiler_params=pltpu.CompilerParams(
+            collective_id=0, has_side_effects=True, vmem_limit_bytes=60 * 2**20),
+    )(activations, projection)
+
+
 def solution(mesh):
+    n_dp, n_mp = mesh.shape["dp"], mesh.shape["mp"]
+
+    def shards(activations, projection):
+        rows, depth = activations.shape
+        width = projection.shape[1]
+        nz = n_dp // 4
+        fits = (
+            n_mp == 2 and n_dp % 8 == 0 and (2 * width) % LANES == 0
+            and depth % LANES == 0 and (depth // 2) % 16 == 0 and rows % (16 * ACT_PIECES) == 0
+            and nz * 2 * 2 * depth * 2 * width * 2 <= 36 * 2**20 and nz <= 4
+        )
+        if fits:
+            return gathered(nz, activations, projection)
+        return general(activations, projection)
+
     placed = (P("dp", "mp"), P("mp", "dp"))
     return jax.shard_map(
         shards, mesh=mesh, in_specs=placed, out_specs=P("dp", "mp"), check_vma=False

time: 268 us -> 147 us (0.55)
  waiting for transfers between devices: 147 us -> 0 us
  Pallas kernels: 0 us -> 137 us
  blocking collectives: 73.6 us -> 0 us
  matrix products: 14.2 us -> 0 us
  between operations: 13.4 us -> 0.01 us
  local copies, waits for them, and re-layouts: 16.7 us -> 7.17 us
    all_gather x2 -> x0, waiting for transfers between devices: 146 us -> none  [the longest x1 130 us: shards(): lax.all_gather(local_cols, 'dp', axis=1, tiled=True)]
    pallas_call x0 -> x1, Pallas kernels: none -> 137 us  [gathered(): pl.pallas_call(functools.partial(kernel, nz), out_shape=jax.ShapeDtypeStr...]
    all_to_all x2 -> x0, blocking collectives: 73.6 us -> none  [the longest x1 56.1 us: shards(): lax.all_to_all(sectioned, 'mp', split_axis=1, concat_axis=2, tiled=True)]
    dot_general x1 -> x0, matrix products: 14.2 us -> none  [shards(): jnp.dot(wide_rows, lax.all_gather(local_cols, 'dp', axis=1, tiled=True),...]
    unnamed x0 -> x2, local copies, waits for them, and re-layouts: none -> 7.17 us
    convert_element_type x1 -> x0, local copies, waits for them, and re-layouts: 6.66 us -> none  [shards(): finished = finished.astype(jnp.bfloat16)]
    reshape x1 -> x0, local copies, waits for them, and re-layouts: 6.61 us -> none  [shards(): return placed.reshape(tok_rows, placed.shape[1] * placed.shape[2] * share)]
    all_to_all x2 -> x0, local copies, waits for them, and re-layouts: 3.48 us -> none  [the longest x1 2.44 us: shards(): lax.all_to_all(sectioned, 'mp', split_axis=1, concat_axis=2, tiled=True)]
  transfers between devices with their start and end apart: 2 -> 0, of which waited for: 2 -> 0; matrix products, arithmetic and copies ran while one was open for 0% -> 0% of each run, Pallas kernels for 0% -> 0%
where the time goes in v1:
time: 147 us; the launch traced here: 145 us
  Pallas kernels  137 us (93%)
  local copies, waits for them, and re-layouts  7.17 us (5%)
    pallas_call x1, Pallas kernels, gathered(): pl.pallas_call(functools.partial(kernel, nz), out_shape=jax.ShapeDtypeStr...  137 us
    unnamed x2, local copies, waits for them, and re-layouts  7.17 us

profile of v1, /device:TPU:3, one launch (start us, length us, event | category | flops | bytes accessed | tf_op | source)
XLA Modules:
  0.0 144.6 jit_solution(11030857063648298563)
XLA Ops:
  0.0 2.3 %copy.3.w_ref = bf16[896,576]{1,0:T(8,128)(2,1)} copy(bf16[896,576]{0,1:T(8,128)(2,1)} %param.3) | data formatting | bytes 2064384 | tf_op args[1]
  2.3 137.4 %shard_map.28 = bf16[512,4608]{1,0:T(8,128)(2,1)} custom-call(bf16[512,896]{1,0:T(8,128)(2,1)} %a_ref.1, bf16[896,576]{1,0:T(8,128)(2,1)} %copy.3.w_ref), custom_call_target="tpu_custom_call" | custom-call | tf_op jit(solution)/shard_map/pallas_call | solution.py:239
  139.7 4.8 %copy.5 = bf16[512,4608]{1,0:T(8,128)(2,1)} copy(bf16[512,4608]{1,0:T(8,128)(2,1)} %shard_map.28) | data formatting | bytes 9437184

commit v2 on v0

v2 whole, which is shorter than its diff:
```python
import functools

import jax
import jax.numpy as jnp
from jax import lax
from jax.experimental import pallas as pl
from jax.experimental.pallas import tpu as pltpu
from jax.sharding import PartitionSpec as P

MESH = pl.DeviceIdType.MESH
LANES = 128
ACT_PIECES = 4
UNIT = 64
DUP = 2
SKEW = 1


def general(activations, projection):
    wide_rows = lax.all_gather(activations, "mp", axis=1, tiled=True)
    local_cols = lax.all_to_all(projection, "mp", split_axis=1, concat_axis=0, tiled=True)
    finished = jnp.dot(
        wide_rows,
        lax.all_gather(local_cols, "dp", axis=1, tiled=True),
        preferred_element_type=jnp.float32,
    )
    finished = finished.astype(jnp.bfloat16)
    tok_rows = finished.shape[0]
    blocks = lax.axis_size("dp")
    share = local_cols.shape[1]
    sectioned = finished.reshape(tok_rows, blocks, 1, share)
    placed = lax.all_to_all(sectioned, "mp", split_axis=1, concat_axis=2, tiled=True)
    return placed.reshape(tok_rows, placed.shape[1] * placed.shape[2] * share)


def kernel(nz, a_ref, w_ref, o_ref, big, acts, outs, send_sem, recv_sem, act_send, act_recv, loc_sem, act_loc, out_sem):
    d, x = lax.axis_index("dp"), lax.axis_index("mp")
    z, y, c = d // 4, (d // 2) % 2, d % 2
    half = nz // 2
    width, depth = w_ref.shape
    rows = a_ref.shape[0]
    steps = width // UNIT
    first_dup = steps - DUP
    per, mid = LANES // UNIT, width // LANES
    loose = (width - mid * LANES) // UNIT
    lag = SKEW * (nz + 2)
    core_dev = (d + 1 - 2 * c, x)
    y_dev = (d + 2 - 4 * y, x)
    x_dev = (d, 1 - x)
    up_dev = (lax.rem(d + 4, 4 * nz), x)
    down_dev = (lax.rem(d + 4 * nz - 4, 4 * nz), x)
    can_up, can_down, never = z < nz - 1, z > 0, z < 0

    def unit_of(cc, t):
        return lax.rem(t + (steps - loose) * (1 - cc), steps)

    def part(zz, yy, xx, cc, t):
        row = pl.multiple_of(cc * width + unit_of(cc, t) * UNIT, UNIT)
        return big.at[zz * 2 + yy, xx, pl.ds(row, UNIT), :]

    def own_copy(t):
        row = pl.multiple_of(unit_of(c, t) * UNIT, UNIT)
        return pltpu.make_async_copy(w_ref.at[pl.ds(row, UNIT), :], part(z, y, x, c, t), loc_sem.at[t])

    own_act = pltpu.make_async_copy(
        a_ref, acts.at[:, pl.ds(pl.multiple_of(x * depth, LANES), depth)], act_loc.at[0])

    def begin(t, carry):
        own_copy(t).start()
        return carry

    lax.fori_loop(0, steps, begin, 0)
    own_act.start()

    barrier = pltpu.get_barrier_semaphore()
    for dev in (core_dev, y_dev, x_dev):
        pl.semaphore_signal(barrier, inc=1, device_id=dev, device_id_type=MESH)

    @pl.when(can_up)
    def _():
        pl.semaphore_signal(barrier, inc=1, device_id=up_dev, device_id_type=MESH)

    @pl.when(can_down)
    def _():
        pl.semaphore_signal(barrier, inc=1, device_id=down_dev, device_id_type=MESH)

    pl.semaphore_wait(barrier, 3 + can_up.astype(jnp.int32) + can_down.astype(jnp.int32))

    def copy(kind, zz, yy, xx, cc, t, dev):
        piece = part(zz, yy, xx, cc, t)
        return pltpu.make_async_remote_copy(
            src_ref=piece, dst_ref=piece, send_sem=send_sem.at[kind, zz, t],
            recv_sem=recv_sem.at[zz, yy, xx * 2 + cc, t], device_id=dev, device_id_type=MESH)

    def along(kind, zz, yy, t, up, down, act):
        @pl.when(up)
        def _():
            act(copy(kind, zz, yy, x, c, t, up_dev))

        @pl.when(down)
        def _():
            act(copy(kind + 1, zz, yy, x, c, t, down_dev))

    def lane_piece(zz, t, up, down, own, act):
        along(0, zz, y, t, up, down, act)
        mine = zz // half == x
        over_y = (t < first_dup) | (t < steps if own else never)

        @pl.when(mine & over_y)
        def _():
            act(copy(2, zz, y, x, c, t, y_dev))

        @pl.when(mine)
        def _():
            act(copy(3, zz, y, x, c, t, core_dev))

        @pl.when(~mine)
        def _():
            act(copy(2, zz, y, x, c, t, x_dev))

        if own:
            @pl.when(~mine & (t >= first_dup))
            def _():
                act(copy(3, zz, y, x, c, t, y_dev))

    def twin_piece(zz, t, up, down, act):
        along(8, zz, 1 - y, t, up, down, act)

        @pl.when(zz // half == x)
        def _():
            act(copy(6, zz, 1 - y, x, c, t, core_dev))

        @pl.when(zz // half != x)
        def _():
            act(copy(6, zz, 1 - y, x, c, t, x_dev))

    def own_stage(t, act, arrive):
        lane_piece(z, t, can_up, can_down, True, act)

    def z_stage(dist, t, act, arrive):
        @pl.when(z >= dist)
        def _():
            arrive(z - dist, y, x, c, t)
            lane_piece(z - dist, t, can_up, never, False, act)

        @pl.when(z + dist < nz)
        def _():
            arrive(z + dist, y, x, c, t)
            lane_piece(z + dist, t, never, can_down, False, act)

    def twin_own_stage(t, act, arrive):
        arrive(z, 1 - y, x, c, t)
        twin_piece(z, t, can_up, can_down, act)

    def twin_z_stage(dist, t, act, arrive):
        @pl.when(z >= dist)
        def _():
            arrive(z - dist, 1 - y, x, c, t)
            twin_piece(z - dist, t, can_up, never, act)

        @pl.when(z + dist < nz)
        def _():
            arrive(z + dist, 1 - y, x, c, t)
            twin_piece(z + dist, t, never, can_down, act)

    def x_stage(h, t, act, arrive):
        zz = x * half + h
        arrive(zz, y, 1 - x, c, t)

        @pl.when(t < first_dup)
        def _():
            act(copy(4, zz, y, 1 - x, c, t, y_dev))

        act(copy(5, zz, y, 1 - x, c, t, core_dev))

    def twin_x_stage(h, t, act, arrive):
        zz = x * half + h
        arrive(zz, 1 - y, 1 - x, c, t)
        act(copy(7, zz, 1 - y, 1 - x, c, t, core_dev))

    def y_stage(h, other, t, act, arrive):
        zz = x * half + h
        xx = 1 - x if other else x
        arrive(zz, 1 - y, xx, c, t)
        act(copy(6 + other, zz, 1 - y, xx, c, t, core_dev))

    def start(cp):
        cp.start()

    def drain(cp):
        cp.wait_send()

    def arrive(zz, yy, xx, cc, t):
        copy(0, zz, yy, xx, cc, t, core_dev).wait_recv()

    def no_arrive(zz, yy, xx, cc, t):
        pass

    act_rows = rows // ACT_PIECES

    def act_copy(k, xx):
        piece = pl.ds(pl.multiple_of(k * act_rows, 16), act_rows)
        return pltpu.make_async_remote_copy(
            src_ref=a_ref.at[piece, :],
            dst_ref=acts.at[piece, pl.ds(pl.multiple_of(xx * depth, LANES), depth)],
            send_sem=act_send.at[k], recv_sem=act_recv.at[k],
            device_id=x_dev, device_id_type=MESH)

    def out_copy(b, g):
        cols = pl.ds(pl.multiple_of(b * 2 * width + g * LANES, LANES), LANES)
        return pltpu.make_async_copy(outs.at[:, cols], o_ref.at[:, cols], out_sem.at[b, g])

    def multiply(g):
        cols = pl.ds(pl.multiple_of(g * LANES, LANES), LANES)
        for b in range(0, 2 * half, 2):
            base = x * 2 * half + b
            rhs = jnp.concatenate([
                jnp.concatenate([big[base + k, 0, cols, :], big[base + k, 1, cols, :]], axis=1)
                for k in range(2)
            ], axis=0)
            res = lax.dot_general(
                acts[...], rhs, (((1,), (1,)), ((), ())), preferred_element_type=jnp.float32
            ).astype(jnp.bfloat16)
            for k in range(2):
                at = pl.ds(pl.multiple_of((b + k) * 2 * width + g * LANES, LANES), LANES)
                outs[:, at] = res[:, k * LANES:(k + 1) * LANES]
                out_copy(b + k, g).start()

    def product(t):
        for h in range(half):
            for yy in range(2):
                for xx in range(2):
                    arrive(x * half + h, yy, xx, 1 - c, t)
        past = t - (loose - 1)
        k = past // per

        def one(j, carry):
            multiply(jnp.where(past == 0, mid, jnp.where(j == 0, k - 1, mid + k)))
            return carry

        @pl.when((past >= 0) & (lax.rem(past + per, per) == 0))
        def _():
            lax.fori_loop(0, jnp.where(past == 0, 1, 2), one, 0)

    def step(i, carry):
        def at(t, stage, low=0, high=steps):
            pl.when((t >= low) & (t < high))(functools.partial(stage, t))

        def go(stage, *lead):
            return lambda t: stage(*lead, t, start, arrive)

        def own(t):
            own_copy(t).wait()
            own_stage(t, start, arrive)

        at(i, own)
        for dist in range(1, nz):
            at(i - SKEW * dist, go(z_stage, dist))
        at(i - SKEW, go(twin_own_stage), first_dup)
        for dist in range(1, nz):
            at(i - SKEW * (1 + dist), go(twin_z_stage, dist), first_dup)

        @pl.when((i >= 1) & (i <= ACT_PIECES))
        def _():
            act_copy(i - 1, x).start()

        @pl.when(i == lag)
        def _():
            own_act.wait()
            for k in range(ACT_PIECES):
                act_copy(k, 1 - x).wait_recv()

        at(i - lag, product)
        for h in range(half):
            away = jnp.abs(z - (x * half + h))
            at(i - SKEW * (away + 1), go(x_stage, h))
            at(i - SKEW * (away + 2), go(twin_x_stage, h), first_dup)
            at(i - SKEW * (away + 1), go(y_stage, h, 0), 0, first_dup)
            at(i - SKEW * (away + 2), go(y_stage, h, 1), 0, first_dup)
        return carry

    lax.fori_loop(0, steps + lag, step, 0)

    def finish(t, carry):
        own_stage(t, drain, no_arrive)
        for dist in range(1, nz):
            z_stage(dist, t, drain, no_arrive)
        for h in range(half):
            x_stage(h, t, drain, no_arrive)

        @pl.when(t < first_dup)
        def _():
            for h in range(half):
                y_stage(h, 0, t, drain, no_arrive)
                y_stage(h, 1, t, drain, no_arrive)

        @pl.when(t >= first_dup)
        def _():
            twin_own_stage(t, drain, no_arrive)
            for dist in range(1, nz):
                twin_z_stage(dist, t, drain, no_arrive)
            for h in range(half):
                twin_x_stage(h, t, drain, no_arrive)

        return carry

    lax.fori_loop(0, steps, finish, 0)
    for k in range(ACT_PIECES):
        act_copy(k, x).wait_send()
    for b in range(2 * half):
        for g in range(2 * width // LANES):
            out_copy(b, g).wait()


def gathered(nz, activations, projection):
    rows, depth = activations.shape
    width = projection.shape[1]
    steps, groups, half = width // UNIT, 2 * width // LANES, nz // 2
    columns = nz * 2 * width
    dma = pltpu.SemaphoreType.DMA
    return pl.pallas_call(
        functools.partial(kernel, nz),
        out_shape=jax.ShapeDtypeStruct((rows, columns), jnp.bfloat16),
        in_specs=[pl.BlockSpec(memory_space=pl.ANY)] * 2,
        out_specs=pl.BlockSpec(memory_space=pl.ANY),
        scratch_shapes=[
            pltpu.VMEM((nz * 2, 2, 2 * width, depth), jnp.bfloat16),
            pltpu.VMEM((rows, 2 * depth), jnp.bfloat16),
            pltpu.VMEM((rows, columns), jnp.bfloat16),
            dma((10, nz, steps)),
            dma((nz, 2, 4, steps)),
            dma((ACT_PIECES,)),
            dma((ACT_PIECES,)),
            dma((steps,)),
            dma((1,)),
            dma((2 * half, groups)),
        ],
        compiler_params=pltpu.CompilerParams(
            collective_id=0, has_side_effects=True, vmem_limit_bytes=60 * 2**20),
    )(activations, projection.T)


def solution(mesh):
    n_dp, n_mp = mesh.shape["dp"], mesh.shape["mp"]

    def shards(activations, projection):
        rows, depth = activations.shape
        width = projection.shape[1]
        nz = n_dp // 4
        fits = (
            n_mp == 2 and n_dp % 8 == 0 and width % LANES == LANES // 2
            and width > LANES and depth % LANES == 0 and rows % (16 * ACT_PIECES) == 0
            and nz * 2 * 2 * depth * 2 * width * 2 <= 36 * 2**20 and nz <= 4
        )
        if fits:
            return gathered(nz, activations, projection)
        return general(activations, projection)

    placed = (P("dp", "mp"), P("mp", "dp"))
    return jax.shard_map(
        shards, mesh=mesh, in_specs=placed, out_specs=P("dp", "mp"), check_vma=False
    )
```

time: 268 us -> 114 us (0.43); the launches traced: 265 us -> 114 us
  waiting for transfers between devices: 147 us -> 0 us
  Pallas kernels: 0 us -> 109 us
  blocking collectives: 73.6 us -> 0 us
  matrix products: 14.2 us -> 0 us
  between operations: 13.4 us -> 0.01 us
  local copies, waits for them, and re-layouts: 16.7 us -> 4.83 us
    all_gather x2 -> x0, waiting for transfers between devices: 146 us -> none  [the longest x1 130 us: shards(): lax.all_gather(local_cols, 'dp', axis=1, tiled=True)]
    pallas_call x0 -> x1, Pallas kernels: none -> 109 us  [gathered(): pl.pallas_call(functools.partial(kernel, nz), out_shape=jax.ShapeDtypeStr...]
    all_to_all x2 -> x0, blocking collectives: 73.6 us -> none  [the longest x1 56.1 us: shards(): lax.all_to_all(sectioned, 'mp', split_axis=1, concat_axis=2, tiled=True)]
    dot_general x1 -> x0, matrix products: 14.2 us -> none  [shards(): jnp.dot(wide_rows, lax.all_gather(local_cols, 'dp', axis=1, tiled=True),...]
    convert_element_type x1 -> x0, local copies, waits for them, and re-layouts: 6.66 us -> none  [shards(): finished = finished.astype(jnp.bfloat16)]
    reshape x1 -> x0, local copies, waits for them, and re-layouts: 6.61 us -> none  [shards(): return placed.reshape(tok_rows, placed.shape[1] * placed.shape[2] * share)]
    unnamed x0 -> x1, local copies, waits for them, and re-layouts: none -> 4.83 us
    all_to_all x2 -> x0, local copies, waits for them, and re-layouts: 3.48 us -> none  [the longest x1 2.44 us: shards(): lax.all_to_all(sectioned, 'mp', split_axis=1, concat_axis=2, tiled=True)]
  transfers between devices with their start and end apart: 2 -> 0, of which waited for: 2 -> 0; matrix products, arithmetic and copies ran while one was open for 0% -> 0% of each run, Pallas kernels for 0% -> 0%
where the time goes in v2:
time: 114 us
  Pallas kernels  109 us (96%)
  local copies, waits for them, and re-layouts  4.83 us (4%)
    pallas_call x1, Pallas kernels, gathered(): pl.pallas_call(functools.partial(kernel, nz), out_shape=jax.ShapeDtypeStr...  109 us
    unnamed x1, local copies, waits for them, and re-layouts  4.83 us

profile of v2, /device:TPU:3, one launch (start us, length us, event | category | flops | bytes accessed | tf_op | source)
XLA Modules:
  0.0 114.2 jit_solution(14110729841912510502)
XLA Ops:
  0.0 109.3 %shard_map.28 = bf16[512,4608]{1,0:T(8,128)(2,1)} custom-call(bf16[512,896]{1,0:T(8,128)(2,1)} %a_ref.1, bf16[576,896]{1,0:T(8,128)(2,1)} %bitcast.1), custom_call_target="tpu_custom_call" | custom-call | tf_op jit(solution)/shard_map/pallas_call | solution.py:320
  109.3 4.8 %copy.4 = bf16[512,4608]{1,0:T(8,128)(2,1)} copy(bf16[512,4608]{1,0:T(8,128)(2,1)} %shard_map.28) | data formatting | bytes 9437184

commit v3 on v2

--- a/solution.py
+++ b/solution.py
@@ -255,9 +255,6 @@
         at(i, own)
         for dist in range(1, nz):
             at(i - SKEW * dist, go(z_stage, dist))
-        at(i - SKEW, go(twin_own_stage), first_dup)
-        for dist in range(1, nz):
-            at(i - SKEW * (1 + dist), go(twin_z_stage, dist), first_dup)
 
         @pl.when((i >= 1) & (i <= ACT_PIECES))
         def _():
@@ -276,6 +273,9 @@
             at(i - SKEW * (away + 2), go(twin_x_stage, h), first_dup)
             at(i - SKEW * (away + 1), go(y_stage, h, 0), 0, first_dup)
             at(i - SKEW * (away + 2), go(y_stage, h, 1), 0, first_dup)
+        at(i - SKEW, go(twin_own_stage), first_dup)
+        for dist in range(1, nz):
+            at(i - SKEW * (1 + dist), go(twin_z_stage, dist), first_dup)
         return carry
 
     lax.fori_loop(0, steps + lag, step, 0)

time: 114 us -> 118 us (1.035)
  Pallas kernels: 109 us -> 113 us
    pallas_call x1, Pallas kernels: 109 us -> 113 us  [gathered(): pl.pallas_call(functools.partial(kernel, nz), out_shape=jax.ShapeDtypeStr...]
where the time goes in v3:
time: 118 us; the launch traced here: 117 us
  Pallas kernels  113 us (96%)
  local copies, waits for them, and re-layouts  4.83 us (4%)
    pallas_call x1, Pallas kernels, gathered(): pl.pallas_call(functools.partial(kernel, nz), out_shape=jax.ShapeDtypeStr...  113 us
    unnamed x1, local copies, waits for them, and re-layouts  4.83 us

profile of v3, /device:TPU:3, one launch (start us, length us, event | category | flops | bytes accessed | tf_op | source)
XLA Modules:
  0.0 117.5 jit_solution(2166806619590344187)
XLA Ops:
  0.0 112.6 %shard_map.28 = bf16[512,4608]{1,0:T(8,128)(2,1)} custom-call(bf16[512,896]{1,0:T(8,128)(2,1)} %a_ref.1, bf16[576,896]{1,0:T(8,128)(2,1)} %bitcast.1), custom_call_target="tpu_custom_call" | custom-call | tf_op jit(solution)/shard_map/pallas_call | solution.py:320
  112.6 4.8 %copy.4 = bf16[512,4608]{1,0:T(8,128)(2,1)} copy(bf16[512,4608]{1,0:T(8,128)(2,1)} %shard_map.28) | data formatting | bytes 9437184
